TPU v7x, 32 devices: a whole 2x2x4 slice. The times are simulated.
32 devices in a mesh: rep: 2 (over x), dp: 16 (over y, z, core).
Axes of the slice: x: 2, y: 2, z: 4, core: 2. Of those that a mesh axis runs over, the one named last changes fastest.
Arguments:
- a: bfloat16 [32, 4, 4096, 1280], P(('rep', 'dp')), parts along dimension 0
- g: bfloat16 [32, 4, 4096, 3072], P(('rep', 'dp')), parts along dimension 0
Outputs:
- output: bfloat16 [8, 1280, 3072], P('rep'), parts along dimension 0
There are 2 independent parts. A program takes and returns all parts, laid end to end along the dimension named above; each array names one.
All inputs are finite; a program needn't handle non-finite values.
Results may differ from a plain program's by a relative error of at most 0.012.
Values are sent between devices in bfloat16 or wider.
A program may use at most 2 GiB of HBM per device.

v0:
```python
import jax
import jax.numpy as jnp


def solution(mesh):
    groups = mesh.shape["rep"]

    def step(a, g):
        a, g = (t.reshape(groups, -1, *t.shape[1:]) for t in (a, g))
        sums = jnp.einsum("rsntd,rsntf->rndf", a, g, preferred_element_type=jnp.float32)
        return sums.astype(jnp.bfloat16).reshape(-1, *sums.shape[2:])

    return step
```

profile of v0, /device:TPU:0, one launch (start us, length us, event | category | flops | bytes accessed | tf_op | source)
XLA Modules:
  0.0 1436.1 jit_solution(6064444900266182570)
XLA Ops:
  0.0 142.3 %fusion.2 = f32[1,4,1280,3072]{3,2,1,0:T(8,128)} fusion(bf16[1,4,4096,3072]{3,2,1,0:T(8,128)(2,1)} %param.1, bf16[1,4,4096,1280]{3,2,1,0:T(8,128)(2,1)} %param), kind=kOutput, calls=%fused_computation.2 | convolution fusion | flops 128849018880 | bytes 205520896 | tf_op jit(solution)/rsntd,rsntf->rndf/dot_general | solution.py:10
  142.3 1293.7 %all-reduce.2 = bf16[1,4,1280,3072]{3,2,1,0:T(8,128)(2,1)} all-reduce(f32[1,4,1280,3072]{3,2,1,0:T(8,128)} %fusion.2), channel_id=1, replica_groups=[2,16]<=[32], use_global_device_ids=true, to_apply=%add.clone | all-reduce | flops 15728640 | bytes 94371840 | tf_op jit(solution)/rsntd,rsntf->rndf/dot_general | solution.py:10
where the time goes:
time: 1440 us
  blocking collectives  1290 us (90%)
  matrix products  142 us (10%)
    dot_general x1, blocking collectives, step(): jnp.einsum('rsntd,rsntf->rndf', a, g, preferred_element_type=jnp.float32)  1290 us
    dot_general x1, matrix products, step(): jnp.einsum('rsntd,rsntf->rndf', a, g, preferred_element_type=jnp.float32)  142 us

commit v1 on v0

v1 whole, which is shorter than its diff:
```python
import jax
import jax.numpy as jnp
from jax import lax
from jax.experimental import pallas as pl
from jax.experimental.pallas import tpu as pltpu
from jax.sharding import PartitionSpec as P

MESH = pl.DeviceIdType.MESH
BF16, F32 = jnp.bfloat16, jnp.float32
W = 256
FIN = 12
DN = (((0,), (0,)), ((), ()))


def kernel(mats, per_mat, a_hbm, g_hbm, out_hbm, a_v, g_v, part, d_s, d_r, y_s, y_r, y_own, za_s, za_r, z_own, zb_s, zb_r,
           zc_s, zc_r, zd_s, zd_r, yz_s, yz_r, fin, a_sem, g_sem, w_sem, sem4s, sem4r, sem8s, sem8r, sem12s, sem12r):
    units = mats * per_mat
    rows = a_v.shape[2]
    half = rows // 2
    q = half // 4
    dp = lax.axis_index("dp")
    y, z, c = dp // 8, (dp // 2) % 4, dp % 2
    mid = jnp.logical_or(z == 1, z == 2)
    end = jnp.logical_not(mid)
    root = jnp.where(z == 2, 1, 0)
    partner = dp + 1 - 2 * c
    yn = dp + 8 - 16 * y
    adj = dp + 2 - 4 * (z % 2)
    om = jnp.where(mid, dp + 6 - 4 * z, dp)

    def at(n):
        return pl.ds(pl.multiple_of(n, 16), q)

    mine = pl.ds(pl.multiple_of(c * half, 16), half)
    theirs = pl.ds(pl.multiple_of((1 - c) * half, 16), half)
    yrow = at(c * half + y * q)
    yrow_other = at(c * half + (1 - y) * q)
    zrow = at(c * half + 2 * q + root * q)
    zrow_other = at(c * half + 2 * q + (1 - root) * q)
    adj_root = jnp.where(z >= 2, 1, 0)
    erow_near = at(c * half + 2 * q + adj_root * q)
    erow_far = at(c * half + 2 * q + (1 - adj_root) * q)

    def rdma(src, dst, ss, rs, to):
        return pltpu.make_async_remote_copy(src_ref=src, dst_ref=dst, send_sem=ss, recv_sem=rs, device_id={"dp": to}, device_id_type=MESH)

    def s4(kind, u):
        return sem4s.at[kind, u % 4], sem4r.at[kind, u % 4]

    def s8(kind, u):
        return sem8s.at[kind, u % 8], sem8r.at[kind, u % 8]

    def s12(kind, u):
        return sem12s.at[kind, u % FIN], sem12r.at[kind, u % FIN]

    d_copy = lambda u: rdma(d_s.at[u % 4], d_r.at[u % 4], *s4(0, u), partner)
    y_copy = lambda u: rdma(y_s.at[u % 4], y_r.at[u % 4], *s4(1, u), yn)
    zc_copy = lambda u: rdma(zc_s.at[u % 4], zc_r.at[u % 4], *s4(2, u), om)
    zd_copy = lambda u: rdma(zd_s.at[u % 4], zd_r.at[u % 4], *s4(3, u), om)
    yz_copy = lambda u: rdma(yz_s.at[u % 4], yz_r.at[u % 4], *s4(4, u), yn)
    za_copy = lambda u: rdma(za_s.at[u % 4], za_r.at[u % 8], *s8(0, u), adj)
    zb_copy = lambda u: rdma(zb_s.at[u % 4], zb_r.at[u % 8], *s8(1, u), adj)

    def fin_copy(kind, r, to):
        return lambda u: rdma(fin.at[u % FIN, r], fin.at[u % FIN, r], *s12(kind, u), to)

    z3_copy = fin_copy(0, yrow, adj)
    near_copy = fin_copy(1, zrow, adj)
    near_in = fin_copy(1, erow_near, adj)
    cross_copy = fin_copy(2, zrow, om)
    cross_in = fin_copy(2, zrow_other, om)
    far_copy = fin_copy(3, zrow_other, adj)
    far_in = fin_copy(3, erow_far, adj)
    ag_copy = fin_copy(4, yrow, yn)
    ag_in = fin_copy(4, yrow_other, yn)
    df_copy = fin_copy(5, mine, partner)
    df_in = fin_copy(5, theirs, partner)

    def out_at(u):
        return out_hbm.at[u // per_mat, :, pl.ds(pl.multiple_of((u % per_mat) * W, W), W)]

    w_copy = lambda u: pltpu.make_async_copy(fin.at[u % FIN], out_at(u), w_sem.at[u % FIN])
    a_copy = lambda n: pltpu.make_async_copy(a_hbm.at[0, n], a_v.at[n % 2], a_sem.at[n % 2])

    def g_copy(u):
        src = g_hbm.at[0, u // per_mat, :, pl.ds(pl.multiple_of((u % per_mat) * W, W), W)]
        return pltpu.make_async_copy(src, g_v.at[u % 3], g_sem.at[u % 3])

    a_copy(0).start()
    g_copy(0).start()
    g_copy(1).start()

    def step(t, _):
        def stage(off):
            u = t - off
            return u, jnp.logical_and(u >= 0, u < units)

        u8, on8 = stage(14)

        @pl.when(on8)
        def _():
            w_copy(u8).wait()

        u7, on7 = stage(12)

        @pl.when(on7)
        def _():
            df_copy(u7).wait_send()
            df_in(u7).wait_recv()
            w_copy(u7).start()

        u6, on6 = stage(11)

        @pl.when(on6)
        def _():
            ag_copy(u6).wait_send()
            ag_in(u6).wait_recv()

            @pl.when(mid)
            def _():
                far_copy(u6).wait_send()

            @pl.when(end)
            def _():
                far_in(u6).wait_recv()

            df_copy(u6).start()

        u5, on5 = stage(9)

        @pl.when(on5)
        def _():
            @pl.when(mid)
            def _():
                cross_in(u5).wait_recv()
                far_copy(u5).start()
                z3_copy(u5).wait_send()
                ag_copy(u5).start()
                near_copy(u5).wait_send()
                cross_copy(u5).wait_send()

            @pl.when(end)
            def _():
                z3_copy(u5).wait_recv()
                ag_copy(u5).start()
                near_in(u5).wait_recv()

        u4, on4 = stage(7)

        @pl.when(jnp.logical_and(on4, mid))
        def _():
            k = u4 % 4
            zd_copy(u4).wait()
            fin[u4 % FIN, yrow, :] = (zd_s[k].astype(F32) + zd_r[k].astype(F32)).astype(BF16)
            z3_copy(u4).start()
            yz_copy(u4).wait()
            fin[u4 % FIN, zrow, :] = (yz_s[k].astype(F32) + yz_r[k].astype(F32)).astype(BF16)
            near_copy(u4).start()
            cross_copy(u4).start()

        u3, on3 = stage(5)

        @pl.when(jnp.logical_and(on3, mid))
        def _():
            k = u3 % 4
            zb_copy(u3).wait_recv()
            zd_s[k] = (y_own[k] + zb_r[u3 % 8].astype(F32)).astype(BF16)
            zd_copy(u3).start()
            zc_copy(u3).wait()
            yz_s[k] = (z_own[k, at(root * q), :] + zc_r[k].astype(F32)).astype(BF16)
            yz_copy(u3).start()

        @pl.when(jnp.logical_and(on3, end))
        def _():
            zb_copy(u3).wait_send()

        u2, on2 = stage(3)

        @pl.when(on2)
        def _():
            k = u2 % 4
            y_copy(u2).wait()

            @pl.when(end)
            def _():
                zb_s[k] = (y_own[k] + y_r[k].astype(F32)).astype(BF16)
                zb_copy(u2).start()
                za_copy(u2).wait_send()

            @pl.when(mid)
            def _():
                y_own[k] = y_own[k] + y_r[k].astype(F32)
                za_copy(u2).wait_recv()
                other = at((1 - root) * q)
                own = at(root * q)
                zc_s[k] = (z_own[k, other, :] + za_r[u2 % 8, other, :].astype(F32)).astype(BF16)
                zc_copy(u2).start()
                z_own[k, own, :] = z_own[k, own, :] + za_r[u2 % 8, own, :].astype(F32)

        @pl.when(t < units)
        def _():
            n = t // per_mat

            @pl.when(t % per_mat == 0)
            def _():
                a_copy(n).wait()

                @pl.when(n + 1 < mats)
                def _():
                    a_copy(n + 1).start()

            g_copy(t).wait()

            @pl.when(t + 2 < units)
            def _():
                g_copy(t + 2).start()

            def block(j, _):
                cols = pl.ds(pl.multiple_of(j * half, 128), half)
                part[t % 2, pl.ds(pl.multiple_of(j * half, 16), half), :] = lax.dot_general(
                    a_v[n % 2, :, cols], g_v[t % 3], DN, preferred_element_type=F32)
                return 0

            lax.fori_loop(0, 2, block, 0)
            d_s[t % 4] = part[t % 2, theirs, :].astype(BF16)
            d_copy(t).start()

        u1, on1 = stage(1)

        @pl.when(on1)
        def _():
            k = u1 % 4
            p = u1 % 2
            d_copy(u1).wait()
            there = (1 - y) * q
            here = y * q
            y_s[k] = (part[p, at(c * half + there), :] + d_r[k, at(there), :].astype(F32)).astype(BF16)
            y_copy(u1).start()
            zpart = pl.ds(pl.multiple_of(c * half + 2 * q, 16), 2 * q)

            @pl.when(end)
            def _():
                za_s[k] = (part[p, zpart, :] + d_r[k, 2 * q:, :].astype(F32)).astype(BF16)
                za_copy(u1).start()

            @pl.when(mid)
            def _():
                z_own[k] = part[p, zpart, :] + d_r[k, 2 * q:, :].astype(F32)

            y_own[k] = part[p, at(c * half + here), :] + d_r[k, at(here), :].astype(F32)

        return 0

    lax.fori_loop(0, units + 15, step, 0)


def solution(mesh):
    def local(a, g):
        _, mats, tokens, rows = a.shape
        cols = g.shape[3]
        half = rows // 2
        q = half // 4

        def buf(slots, n, dtype=BF16):
            return pltpu.VMEM((slots, n, W), dtype)

        def body(*refs):
            kernel(mats, cols // W, *refs)

        any_spec = pl.BlockSpec(memory_space=pl.ANY)
        dma = pltpu.SemaphoreType.DMA
        return pl.pallas_call(
            body,
            out_shape=jax.ShapeDtypeStruct((mats, rows, cols), BF16),
            in_specs=[any_spec, any_spec],
            out_specs=any_spec,
            scratch_shapes=[
                pltpu.VMEM((2, tokens, rows), BF16),
                pltpu.VMEM((3, tokens, W), BF16),
                buf(2, rows, F32),
                buf(4, half), buf(4, half),
                buf(4, q), buf(4, q), buf(4, q, F32),
                buf(4, 2 * q), buf(8, 2 * q), buf(4, 2 * q, F32),
                buf(4, q), buf(8, q),
                buf(4, q), buf(4, q),
                buf(4, q), buf(4, q),
                buf(4, q), buf(4, q),
                buf(FIN, rows),
                dma((2,)), dma((3,)), dma((FIN,)),
                dma((5, 4)), dma((5, 4)),
                dma((2, 8)), dma((2, 8)),
                dma((6, FIN)), dma((6, FIN)),
            ],
            compiler_params=pltpu.CompilerParams(has_side_effects=True, vmem_limit_bytes=60 * 2**20),
            cost_estimate=pl.CostEstimate(flops=2 * mats * tokens * rows * cols, bytes_accessed=2 * mats * tokens * (rows + cols), transcendentals=0),
        )(a, g)

    spec = P(("rep", "dp"))
    return jax.shard_map(local, mesh=mesh, in_specs=(spec, spec), out_specs=P("rep"), check_vma=False)
```

time: 1440 us -> 326 us (0.23)
  blocking collectives: 1290 us -> 0 us
  Pallas kernels: 0 us -> 305 us
  matrix products: 142 us -> 0 us
  local copies, waits for them, and re-layouts: 0 us -> 21.5 us
    dot_general x1 -> x0, blocking collectives: 1290 us -> none  [step(): jnp.einsum('rsntd,rsntf->rndf', a, g, preferred_element_type=jnp.float32)]
    pallas_call x0 -> x1, Pallas kernels: none -> 305 us  [local(): pl.pallas_call(body, out_shape=jax.ShapeDtypeStruct((mats, rows, cols), B...]
    dot_general x1 -> x0, matrix products: 142 us -> none  [step(): jnp.einsum('rsntd,rsntf->rndf', a, g, preferred_element_type=jnp.float32)]
    unnamed x0 -> x1, local copies, waits for them, and re-layouts: none -> 21.5 us
where the time goes in v1:
time: 326 us
  Pallas kernels  305 us (94%)
  local copies, waits for them, and re-layouts  21.5 us (7%)
    pallas_call x1, Pallas kernels, local(): pl.pallas_call(body, out_shape=jax.ShapeDtypeStruct((mats, rows, cols), B...  305 us
    unnamed x1, local copies, waits for them, and re-layouts  21.5 us

profile of v1, /device:TPU:0, one launch (start us, length us, event | category | flops | bytes accessed | tf_op | source)
XLA Modules:
  0.0 326.0 jit_solution(15444337415466625723)
XLA Ops:
  0.0 304.6 %shard_map.28 = bf16[4,1280,3072]{2,1,0:T(8,128)(2,1)} custom-call(bf16[1,4,4096,1280]{3,2,1,0:T(8,128)(2,1)} %refs_0_.1, bf16[1,4,4096,3072]{3,2,1,0:T(8,128)(2,1)} %refs_1_.1), custom_call_target="tpu_custom_call" | custom-call | flops 128849018880 | bytes 142606336 | tf_op jit(solution)/shard_map/pallas_call | solution.py:272
  304.6 21.5 %copy.4 = bf16[4,1280,3072]{2,1,0:T(8,128)(2,1)} copy(bf16[4,1280,3072]{2,1,0:T(8,128)(2,1)} %shard_map.28) | data formatting | bytes 62914560

commit v2 on v0

v2 whole, which is shorter than its diff:
```python
import jax
import jax.numpy as jnp
from jax import lax
from jax.experimental import pallas as pl
from jax.experimental.pallas import tpu as pltpu
from jax.sharding import PartitionSpec as P

MESH = pl.DeviceIdType.MESH
BF16, F32 = jnp.bfloat16, jnp.float32
W = 256
PARTS = 2
SLOTS = 8
LAG = 2
DN = (((0,), (0,)), ((), ()))


def kernel(mats, q, zq, a_hbm, g_hbm, out, a_v, g_v, part, d_s, d_r, y_s, y_r, y_own, za_s, za_r, z_own, zb_s, zb_r,
           zm_s, zm_r, zd_s, zd_r, ze_s, ze_r, yz_s, yz_r, a_sem, g_sem, send_sem, recv_sem):
    rows = a_v.shape[2]
    half = rows // 2
    per_row = out.shape[2] // W
    units = mats * PARTS * per_row
    dp = lax.axis_index("dp")
    y, z, c = dp // 8, (dp // 2) % 4, dp % 2
    mid = jnp.logical_or(z == 1, z == 2)
    end = jnp.logical_not(mid)
    side = z // 2
    partner = dp + 1 - 2 * c
    yn = dp + 8 - 16 * y
    adj = dp + 2 - 4 * (z % 2)
    om = jnp.where(mid, dp + 6 - 4 * z, dp)
    r_adj = z + 1 - 2 * (z % 2)
    r_om = 3 - z
    r_far = r_om + 1 - 2 * (r_om % 2)

    def span(start, n):
        return pl.ds(pl.multiple_of(start, 16), n)

    def rdma(kind, src, dst, u, to):
        return pltpu.make_async_remote_copy(
            src_ref=src, dst_ref=dst, send_sem=send_sem.at[kind, u % SLOTS], recv_sem=recv_sem.at[kind, u % SLOTS],
            device_id={"dp": to}, device_id_type=MESH)

    def place(u):
        n = u // (PARTS * per_row)
        return n, (u // per_row) % PARTS, pl.ds(pl.multiple_of((u % per_row) * W, W), W)

    def out_at(u, core, start, n):
        m, p, cols = place(u)
        return out.at[m, span(p * rows + core * half + start, n), cols]

    def final_copy(kind, core, start, n, to):
        def make(u):
            ref = out_at(u, core, start, n)
            return rdma(kind, ref, ref, u, to)

        return make

    def piece(r):
        return 2 * q + r * zq

    d_copy = lambda u: rdma(0, d_s.at[u % 4], d_r.at[u % SLOTS], u, partner)
    y_copy = lambda u: rdma(1, y_s.at[u % 4], y_r.at[u % SLOTS], u, yn)
    near_rows = span((1 - side) * zq, 3 * zq)
    za_copy = lambda u: rdma(2, za_s.at[u % 4], za_r.at[u % SLOTS, near_rows], u, adj)
    zb_copy = lambda u: rdma(3, zb_s.at[u % 4], zb_r.at[u % SLOTS], u, adj)
    zm_copy = lambda u: rdma(4, zm_s.at[u % 4], zm_r.at[u % SLOTS], u, om)
    zd_copy = lambda u: rdma(5, zd_s.at[u % 4], zd_r.at[u % SLOTS], u, om)
    ze_copy = lambda u: rdma(6, ze_s.at[u % 4], ze_r.at[u % SLOTS], u, adj)
    yz_copy = lambda u: rdma(7, yz_s.at[u % 4], yz_r.at[u % SLOTS], u, yn)
    z3_copy = final_copy(8, c, y * q, q, adj)
    ag_copy = final_copy(9, c, y * q, q, yn)
    ag_in = final_copy(9, c, (1 - y) * q, q, yn)
    near_copy = final_copy(10, c, piece(z), zq, adj)
    near_in = final_copy(10, c, piece(r_adj), zq, adj)
    cross_copy = final_copy(11, c, piece(z), zq, om)
    cross_in = final_copy(11, c, piece(r_om), zq, om)
    up_copy = final_copy(12, c, piece(z), zq, adj)
    up_in = final_copy(12, c, piece(r_adj), zq, adj)
    far1_copy = final_copy(13, c, piece(r_om), zq, adj)
    far1_in = final_copy(13, c, piece(r_far), zq, adj)
    over_copy = final_copy(14, c, piece(r_adj), zq, om)
    over_in = final_copy(14, c, piece(r_far), zq, om)
    far2_copy = final_copy(15, c, piece(r_far), zq, adj)
    far2_in = final_copy(15, c, piece(r_om), zq, adj)
    df_copy = final_copy(16, c, 0, half, partner)
    df_in = final_copy(16, 1 - c, 0, half, partner)

    def a_copy(i):
        src = a_hbm.at[0, i // PARTS, :, pl.ds(pl.multiple_of((i % PARTS) * rows, 128), rows)]
        return pltpu.make_async_copy(src, a_v.at[i % 2], a_sem.at[i % 2])

    def g_copy(u):
        m, _, cols = place(u)
        return pltpu.make_async_copy(g_hbm.at[0, m, :, cols], g_v.at[u % 3], g_sem.at[u % 3])

    def store(u, start, n, value):
        m, p, cols = place(u)
        out[m, span(p * rows + c * half + start, n), cols] = value.astype(BF16)

    a_copy(0).start()
    g_copy(0).start()
    g_copy(1).start()

    def step(t, _):
        def stage(off, who=None):
            u = t - off
            on = jnp.logical_and(u >= 0, u < units)
            return u, pl.when(on if who is None else jnp.logical_and(on, who))

        u, when = stage(2 + 7 * LAG)

        @when
        def _(u=u):
            df_copy(u).wait_send()
            df_in(u).wait_recv()

        u, when = stage(1 + 7 * LAG, mid)

        @when
        def _(u=u):
            far2_copy(u).wait_send()
            df_copy(u).start()

        u, when = stage(1 + 7 * LAG, end)

        @when
        def _(u=u):
            far2_in(u).wait_recv()
            df_copy(u).start()

        u, when = stage(1 + 6 * LAG, mid)

        @when
        def _(u=u):
            over_in(u).wait_recv()
            far2_copy(u).start()
            over_copy(u).wait_send()

        u, when = stage(1 + 5 * LAG)

        @when
        def _(u=u):
            @pl.when(mid)
            def _():
                up_in(u).wait_recv()
                over_copy(u).start()
                far1_copy(u).wait_send()

            @pl.when(end)
            def _():
                far1_in(u).wait_recv()
                up_copy(u).wait_send()

            ag_copy(u).wait_send()
            ag_in(u).wait_recv()

        u, when = stage(1 + 4 * LAG, mid)

        @when
        def _(u=u):
            z3_copy(u).wait_send()
            ag_copy(u).start()
            cross_in(u).wait_recv()
            far1_copy(u).start()
            near_copy(u).wait_send()
            cross_copy(u).wait_send()

        u, when = stage(1 + 4 * LAG, end)

        @when
        def _(u=u):
            z3_copy(u).wait_recv()
            ag_copy(u).start()
            yz_copy(u).wait()
            store(u, piece(z), zq, yz_s[u % 4].astype(F32) + yz_r[u % SLOTS].astype(F32))
            up_copy(u).start()
            near_in(u).wait_recv()

        u, when = stage(1 + 3 * LAG, mid)

        @when
        def _(u=u):
            zd_copy(u).wait()
            store(u, y * q, q, zd_s[u % 4].astype(F32) + zd_r[u % SLOTS].astype(F32))
            z3_copy(u).start()
            yz_copy(u).wait()
            store(u, piece(z), zq, yz_s[u % 4].astype(F32) + yz_r[u % SLOTS].astype(F32))
            near_copy(u).start()
            cross_copy(u).start()
            ze_copy(u).wait_send()

        u, when = stage(1 + 3 * LAG, end)

        @when
        def _(u=u):
            ze_copy(u).wait_recv()
            k = u % SLOTS
            yz_s[u % 4] = (z_own[k, span(z * zq, zq)] + ze_r[k].astype(F32)).astype(BF16)
            yz_copy(u).start()

        u, when = stage(1 + 2 * LAG, mid)

        @when
        def _(u=u):
            k = u % SLOTS
            zb_copy(u).wait_recv()
            zd_s[u % 4] = (y_own[k] + zb_r[k].astype(F32)).astype(BF16)
            zd_copy(u).start()
            zm_copy(u).wait()
            ze_s[u % 4] = (z_own[k, span(r_adj * zq, zq)] + zm_r[k, span((r_adj % 2) * zq, zq)].astype(F32)).astype(BF16)
            ze_copy(u).start()
            mine = span(z * zq, zq)
            yz_s[u % 4] = (z_own[k, mine] + za_r[k, mine].astype(F32) + zm_r[k, span((z % 2) * zq, zq)].astype(F32)).astype(BF16)
            yz_copy(u).start()

        u, when = stage(1 + 2 * LAG, end)

        @when
        def _(u=u):
            zb_copy(u).wait_send()

        u, when = stage(1 + LAG)

        @when
        def _(u=u):
            k = u % SLOTS
            y_copy(u).wait()

            @pl.when(end)
            def _():
                zb_s[u % 4] = (y_own[k] + y_r[k].astype(F32)).astype(BF16)
                zb_copy(u).start()
                za_copy(u).wait_send()

            @pl.when(mid)
            def _():
                za_copy(u).wait_recv()
                other = span((1 - side) * 2 * zq, 2 * zq)
                zm_s[u % 4] = (z_own[k, other] + za_r[k, other].astype(F32)).astype(BF16)
                zm_copy(u).start()
                y_own[k] = y_own[k] + y_r[k].astype(F32)

        @pl.when(t < units)
        def _():
            i = t // per_row

            @pl.when(t % per_row == 0)
            def _():
                a_copy(i).wait()

                @pl.when(i + 1 < mats * PARTS)
                def _():
                    a_copy(i + 1).start()

            g_copy(t).wait()

            @pl.when(t + 2 < units)
            def _():
                g_copy(t + 2).start()

            part[t % 2] = lax.dot_general(a_v[i % 2], g_v[t % 3], DN, preferred_element_type=F32)
            d_s[t % 4] = part[t % 2, span((1 - c) * half, half), :].astype(BF16)
            d_copy(t).start()

        u, when = stage(1)

        @when
        def _(u=u):
            k = u % SLOTS
            p = u % 2
            d_copy(u).wait()
            there = (1 - y) * q
            here = y * q
            y_s[u % 4] = (part[p, span(c * half + there, q)] + d_r[k, span(there, q)].astype(F32)).astype(BF16)
            y_copy(u).start()

            @pl.when(end)
            def _():
                start = 2 * q + (1 - side) * zq
                za_s[u % 4] = (part[p, span(c * half + start, 3 * zq)] + d_r[k, span(start, 3 * zq)].astype(F32)).astype(BF16)
                za_copy(u).start()

            y_own[k] = part[p, span(c * half + here, q)] + d_r[k, span(here, q)].astype(F32)
            z_own[k] = part[p, span(c * half + 2 * q, 4 * zq)] + d_r[k, 2 * q:].astype(F32)

        return 0

    lax.fori_loop(0, units + 3 + 7 * LAG, step, 0)


def write(x, out, sems):
    copies = [pltpu.make_async_copy(x.at[n], out.at[n], sems.at[n]) for n in range(out.shape[0])]
    for copy in copies:
        copy.start()
    for copy in copies:
        copy.wait()


def solution(mesh):
    def local(a, g):
        _, mats, tokens, depth = a.shape
        cols = g.shape[3]
        rows = depth // PARTS
        half = rows // 2
        zq = half // 10
        q = 3 * zq

        def buf(slots, n, dtype=BF16):
            return pltpu.VMEM((slots, n, W), dtype)

        def body(*refs):
            kernel(mats, q, zq, *refs)

        any_spec = pl.BlockSpec(memory_space=pl.ANY)
        dma = pltpu.SemaphoreType.DMA
        sums = pl.pallas_call(
            body,
            out_shape=pltpu.VMEM((mats, depth, cols), BF16),
            in_specs=[any_spec, any_spec],
            out_specs=pl.BlockSpec(memory_space=pltpu.VMEM),
            scratch_shapes=[
                pltpu.VMEM((2, tokens, rows), BF16),
                pltpu.VMEM((3, tokens, W), BF16),
                buf(2, rows, F32),
                buf(4, half), buf(SLOTS, half),
                buf(4, q), buf(SLOTS, q), buf(SLOTS, q, F32),
                buf(4, 3 * zq), buf(SLOTS, 4 * zq), buf(SLOTS, 4 * zq, F32),
                buf(4, q), buf(SLOTS, q),
                buf(4, 2 * zq), buf(SLOTS, 2 * zq),
                buf(4, q), buf(SLOTS, q),
                buf(4, zq), buf(SLOTS, zq),
                buf(4, zq), buf(SLOTS, zq),
                dma((2,)), dma((3,)),
                dma((17, SLOTS)), dma((17, SLOTS)),
            ],
            compiler_params=pltpu.CompilerParams(has_side_effects=True, vmem_limit_bytes=31 * 2**20),
            cost_estimate=pl.CostEstimate(flops=2 * mats * tokens * depth * cols, bytes_accessed=2 * mats * tokens * (depth + cols), transcendentals=0),
        )(a, g)
        return pl.pallas_call(
            write,
            out_shape=jax.ShapeDtypeStruct((mats, depth, cols), BF16),
            in_specs=[any_spec],
            out_specs=any_spec,
            scratch_shapes=[dma((mats,))],
            compiler_params=pltpu.CompilerParams(vmem_limit_bytes=2**20),
        )(sums)

    spec = P(("rep", "dp"))
    return jax.shard_map(local, mesh=mesh, in_specs=(spec, spec), out_specs=P("rep"), check_vma=False)
```

time: 1440 us -> 287 us (0.20)
  blocking collectives: 1290 us -> 0 us
  Pallas kernels: 0 us -> 287 us
  matrix products: 142 us -> 0 us
    dot_general x1 -> x0, blocking collectives: 1290 us -> none  [step(): jnp.einsum('rsntd,rsntf->rndf', a, g, preferred_element_type=jnp.float32)]
    pallas_call x0 -> x2, Pallas kernels: none -> 287 us  [the longest x1 277 us: local(): pl.pallas_call(body, out_shape=pltpu.VMEM((mats, depth, cols), BF16), in_...]
    dot_general x1 -> x0, matrix products: 142 us -> none  [step(): jnp.einsum('rsntd,rsntf->rndf', a, g, preferred_element_type=jnp.float32)]
where the time goes in v2:
time: 287 us
  Pallas kernels  287 us (100%)
    pallas_call x1, Pallas kernels, local(): pl.pallas_call(body, out_shape=pltpu.VMEM((mats, depth, cols), BF16), in_...  277 us
    pallas_call x1, Pallas kernels, local(): pl.pallas_call(write, out_shape=jax.ShapeDtypeStruct((mats, depth, cols),...  10.6 us

profile of v2, /device:TPU:0, one launch (start us, length us, event | category | flops | bytes accessed | tf_op | source)
XLA Modules:
  0.0 287.2 jit_solution(6005168883011998167)
XLA Ops:
  0.0 276.6 %shard_map.28.x = bf16[4,1280,3072]{2,1,0:T(8,128)(2,1)S(1)} custom-call(bf16[1,4,4096,1280]{3,2,1,0:T(8,128)(2,1)} %refs_0_.1, bf16[1,4,4096,3072]{3,2,1,0:T(8,128)(2,1)} %refs_1_.1), custom_call_target="tpu_custom_call" | custom-call | flops 128849018880 | bytes 142606336 | tf_op jit(solution)/shard_map/pallas_call | solution.py:317
  276.6 10.6 %shard_map.29 = bf16[4,1280,3072]{2,1,0:T(8,128)(2,1)} custom-call(bf16[4,1280,3072]{2,1,0:T(8,128)(2,1)S(1)} %shard_map.28.x), custom_call_target="tpu_custom_call" | custom-call | tf_op jit(solution)/shard_map/pallas_call | solution.py:340

commit v3 on v2

--- a/solution.py
+++ b/solution.py
@@ -10,12 +10,16 @@
 W = 256
 PARTS = 2
 SLOTS = 8
+SEMS = 16
+LATE = 3
+CHUNKS = 4
 LAG = 2
+WRITES = 4
 DN = (((0,), (0,)), ((), ()))
 
 
 def kernel(mats, q, zq, a_hbm, g_hbm, out, a_v, g_v, part, d_s, d_r, y_s, y_r, y_own, za_s, za_r, z_own, zb_s, zb_r,
-           zm_s, zm_r, zd_s, zd_r, ze_s, ze_r, yz_s, yz_r, a_sem, g_sem, send_sem, recv_sem):
+           zm_s, zm_r, zd_s, zd_r, ze_s, ze_r, yz_s, yz_r, a_sem, g_sem, first_sem, send_sem, recv_sem):
     rows = a_v.shape[2]
     half = rows // 2
     per_row = out.shape[2] // W
@@ -33,12 +37,15 @@
     r_om = 3 - z
     r_far = r_om + 1 - 2 * (r_om % 2)
 
+    far_mid = dp + 2 * (r_far - z)
+    far_end = dp + 2 * (r_om - z)
+
     def span(start, n):
         return pl.ds(pl.multiple_of(start, 16), n)
 
     def rdma(kind, src, dst, u, to):
         return pltpu.make_async_remote_copy(
-            src_ref=src, dst_ref=dst, send_sem=send_sem.at[kind, u % SLOTS], recv_sem=recv_sem.at[kind, u % SLOTS],
+            src_ref=src, dst_ref=dst, send_sem=send_sem.at[kind, u % SEMS], recv_sem=recv_sem.at[kind, u % SEMS],
             device_id={"dp": to}, device_id_type=MESH)
 
     def place(u):
@@ -83,6 +90,8 @@
     over_in = final_copy(14, c, piece(r_far), zq, om)
     far2_copy = final_copy(15, c, piece(r_far), zq, adj)
     far2_in = final_copy(15, c, piece(r_om), zq, adj)
+    over_late = final_copy(14, c, piece(z), zq, far_mid)
+    far2_late = final_copy(15, c, piece(z), zq, far_end)
     df_copy = final_copy(16, c, 0, half, partner)
     df_in = final_copy(16, 1 - c, 0, half, partner)
 
@@ -98,9 +107,24 @@
         m, p, cols = place(u)
         out[m, span(p * rows + c * half + start, n), cols] = value.astype(BF16)
 
-    a_copy(0).start()
-    g_copy(0).start()
+    tokens = a_v.shape[1] // CHUNKS
+
+    def first_copies(i):
+        some = span(i * tokens, tokens)
+        return (pltpu.make_async_copy(a_hbm.at[0, 0, some, pl.ds(0, rows)], a_v.at[0, some], first_sem.at[0, i]),
+                pltpu.make_async_copy(g_hbm.at[0, 0, some, pl.ds(0, W)], g_v.at[0, some], first_sem.at[1, i]))
+
+    for i in range(CHUNKS):
+        for copy in first_copies(i):
+            copy.start()
+    a_copy(1).start()
     g_copy(1).start()
+
+    barrier = pltpu.get_barrier_semaphore()
+    peers = [partner, yn] + [dp + 2 * ((z + i) % 4 - z) for i in range(1, 4)]
+    for peer in peers:
+        pl.semaphore_signal(barrier, inc=1, device_id={"dp": peer}, device_id_type=MESH)
+    pl.semaphore_wait(barrier, len(peers))
 
     def step(t, _):
         def stage(off, who=None):
@@ -119,7 +143,10 @@
 
         @when
         def _(u=u):
-            far2_copy(u).wait_send()
+            @pl.when(u < units - LATE)
+            def _():
+                far2_copy(u).wait_send()
+
             df_copy(u).start()
 
         u, when = stage(1 + 7 * LAG, end)
@@ -134,8 +161,11 @@
         @when
         def _(u=u):
             over_in(u).wait_recv()
-            far2_copy(u).start()
-            over_copy(u).wait_send()
+
+            @pl.when(u < units - LATE)
+            def _():
+                far2_copy(u).start()
+                over_copy(u).wait_send()
 
         u, when = stage(1 + 5 * LAG)
 
@@ -144,13 +174,22 @@
             @pl.when(mid)
             def _():
                 up_in(u).wait_recv()
-                over_copy(u).start()
+
+                @pl.when(u < units - LATE)
+                def _():
+                    over_copy(u).start()
+
                 far1_copy(u).wait_send()
 
             @pl.when(end)
             def _():
                 far1_in(u).wait_recv()
                 up_copy(u).wait_send()
+
+                @pl.when(u >= units - LATE)
+                def _():
+                    over_late(u).wait_send()
+                    far2_late(u).wait_send()
 
             ag_copy(u).wait_send()
             ag_in(u).wait_recv()
@@ -175,6 +214,12 @@
             yz_copy(u).wait()
             store(u, piece(z), zq, yz_s[u % 4].astype(F32) + yz_r[u % SLOTS].astype(F32))
             up_copy(u).start()
+
+            @pl.when(u >= units - LATE)
+            def _():
+                over_late(u).start()
+                far2_late(u).start()
+
             near_in(u).wait_recv()
 
         u, when = stage(1 + 3 * LAG, mid)
@@ -245,7 +290,7 @@
         def _():
             i = t // per_row
 
-            @pl.when(t % per_row == 0)
+            @pl.when(jnp.logical_and(t % per_row == 0, t > 0))
             def _():
                 a_copy(i).wait()
 
@@ -253,13 +298,27 @@
                 def _():
                     a_copy(i + 1).start()
 
-            g_copy(t).wait()
-
             @pl.when(t + 2 < units)
             def _():
                 g_copy(t + 2).start()
 
-            part[t % 2] = lax.dot_general(a_v[i % 2], g_v[t % 3], DN, preferred_element_type=F32)
+            @pl.when(t == 0)
+            def _():
+                def chunk(i, _):
+                    for copy in first_copies(i):
+                        copy.wait()
+                    some = span(i * tokens, tokens)
+                    more = lax.dot_general(a_v[0, some], g_v[0, some], DN, preferred_element_type=F32)
+                    part[0] = jnp.where(i == 0, more, part[0] + more)
+                    return 0
+
+                lax.fori_loop(0, CHUNKS, chunk, 0)
+
+            @pl.when(t > 0)
+            def _():
+                g_copy(t).wait()
+                part[t % 2] = lax.dot_general(a_v[i % 2], g_v[t % 3], DN, preferred_element_type=F32)
+
             d_s[t % 4] = part[t % 2, span((1 - c) * half, half), :].astype(BF16)
             d_copy(t).start()
 
@@ -290,7 +349,10 @@
 
 
 def write(x, out, sems):
-    copies = [pltpu.make_async_copy(x.at[n], out.at[n], sems.at[n]) for n in range(out.shape[0])]
+    mats, rows, _ = out.shape
+    part = rows // WRITES
+    copies = [pltpu.make_async_copy(x.at[n, pl.ds(i * part, part)], out.at[n, pl.ds(i * part, part)], sems.at[n, i])
+              for n in range(mats) for i in range(WRITES)]
     for copy in copies:
         copy.start()
     for copy in copies:
@@ -331,10 +393,10 @@
                 buf(4, q), buf(SLOTS, q),
                 buf(4, zq), buf(SLOTS, zq),
                 buf(4, zq), buf(SLOTS, zq),
-                dma((2,)), dma((3,)),
-                dma((17, SLOTS)), dma((17, SLOTS)),
+                dma((2,)), dma((3,)), dma((2, CHUNKS)),
+                dma((17, SEMS)), dma((17, SEMS)),
             ],
-            compiler_params=pltpu.CompilerParams(has_side_effects=True, vmem_limit_bytes=31 * 2**20),
+            compiler_params=pltpu.CompilerParams(collective_id=0, has_side_effects=True, vmem_limit_bytes=31 * 2**20),
             cost_estimate=pl.CostEstimate(flops=2 * mats * tokens * depth * cols, bytes_accessed=2 * mats * tokens * (depth + cols), transcendentals=0),
         )(a, g)
         return pl.pallas_call(
@@ -342,7 +404,7 @@
             out_shape=jax.ShapeDtypeStruct((mats, depth, cols), BF16),
             in_specs=[any_spec],
             out_specs=any_spec,
-            scratch_shapes=[dma((mats,))],
+            scratch_shapes=[dma((mats, WRITES))],
             compiler_params=pltpu.CompilerParams(vmem_limit_bytes=2**20),
         )(sums)
 

time: 287 us -> 282 us (0.983)
  Pallas kernels: 287 us -> 282 us
    pallas_call x1, Pallas kernels: 277 us -> 272 us  [local(): pl.pallas_call(body, out_shape=pltpu.VMEM((mats, depth, cols), BF16), in_...]
where the time goes in v3:
time: 282 us
  Pallas kernels  282 us (100%)
    pallas_call x1, Pallas kernels, local(): pl.pallas_call(body, out_shape=pltpu.VMEM((mats, depth, cols), BF16), in_...  272 us
    pallas_call x1, Pallas kernels, local(): pl.pallas_call(write, out_shape=jax.ShapeDtypeStruct((mats, depth, cols),...  10.4 us

profile of v3, /device:TPU:0, one launch (start us, length us, event | category | flops | bytes accessed | tf_op | source)
XLA Modules:
  0.0 282.0 jit_solution(14735673800359438920)
XLA Ops:
  0.0 271.6 %shard_map.28.x = bf16[4,1280,3072]{2,1,0:T(8,128)(2,1)S(1)} custom-call(bf16[1,4,4096,1280]{3,2,1,0:T(8,128)(2,1)} %refs_0_.1, bf16[1,4,4096,3072]{3,2,1,0:T(8,128)(2,1)} %refs_1_.1), custom_call_target="tpu_custom_call" | custom-call | flops 128849018880 | bytes 142606336 | tf_op jit(solution)/shard_map/pallas_call | solution.py:379
  271.6 10.4 %shard_map.29 = bf16[4,1280,3072]{2,1,0:T(8,128)(2,1)} custom-call(bf16[4,1280,3072]{2,1,0:T(8,128)(2,1)S(1)} %shard_map.28.x), custom_call_target="tpu_custom_call" | custom-call | tf_op jit(solution)/shard_map/pallas_call | solution.py:402

commit v4 on v3

--- a/solution.py
+++ b/solution.py
@@ -11,7 +11,7 @@
 PARTS = 2
 SLOTS = 8
 SEMS = 16
-LATE = 3
+LATE = 2
 CHUNKS = 4
 LAG = 2
 WRITES = 4
@@ -132,14 +132,14 @@
             on = jnp.logical_and(u >= 0, u < units)
             return u, pl.when(on if who is None else jnp.logical_and(on, who))
 
-        u, when = stage(2 + 7 * LAG)
+        u, when = stage(3 + 7 * LAG)
 
         @when
         def _(u=u):
             df_copy(u).wait_send()
             df_in(u).wait_recv()
 
-        u, when = stage(1 + 7 * LAG, mid)
+        u, when = stage(2 + 7 * LAG, mid)
 
         @when
         def _(u=u):
@@ -149,14 +149,14 @@
 
             df_copy(u).start()
 
-        u, when = stage(1 + 7 * LAG, end)
+        u, when = stage(2 + 7 * LAG, end)
 
         @when
         def _(u=u):
             far2_in(u).wait_recv()
             df_copy(u).start()
 
-        u, when = stage(1 + 6 * LAG, mid)
+        u, when = stage(2 + 6 * LAG, mid)
 
         @when
         def _(u=u):
@@ -167,7 +167,7 @@
                 far2_copy(u).start()
                 over_copy(u).wait_send()
 
-        u, when = stage(1 + 5 * LAG)
+        u, when = stage(2 + 5 * LAG)
 
         @when
         def _(u=u):
@@ -194,7 +194,7 @@
             ag_copy(u).wait_send()
             ag_in(u).wait_recv()
 
-        u, when = stage(1 + 4 * LAG, mid)
+        u, when = stage(2 + 4 * LAG, mid)
 
         @when
         def _(u=u):
@@ -205,7 +205,7 @@
             near_copy(u).wait_send()
             cross_copy(u).wait_send()
 
-        u, when = stage(1 + 4 * LAG, end)
+        u, when = stage(2 + 4 * LAG, end)
 
         @when
         def _(u=u):
@@ -222,7 +222,7 @@
 
             near_in(u).wait_recv()
 
-        u, when = stage(1 + 3 * LAG, mid)
+        u, when = stage(2 + 3 * LAG, mid)
 
         @when
         def _(u=u):
@@ -235,7 +235,7 @@
             cross_copy(u).start()
             ze_copy(u).wait_send()
 
-        u, when = stage(1 + 3 * LAG, end)
+        u, when = stage(2 + 3 * LAG, end)
 
         @when
         def _(u=u):
@@ -244,7 +244,7 @@
             yz_s[u % 4] = (z_own[k, span(z * zq, zq)] + ze_r[k].astype(F32)).astype(BF16)
             yz_copy(u).start()
 
-        u, when = stage(1 + 2 * LAG, mid)
+        u, when = stage(2 + 2 * LAG, mid)
 
         @when
         def _(u=u):
@@ -259,13 +259,13 @@
             yz_s[u % 4] = (z_own[k, mine] + za_r[k, mine].astype(F32) + zm_r[k, span((z % 2) * zq, zq)].astype(F32)).astype(BF16)
             yz_copy(u).start()
 
-        u, when = stage(1 + 2 * LAG, end)
+        u, when = stage(2 + 2 * LAG, end)
 
         @when
         def _(u=u):
             zb_copy(u).wait_send()
 
-        u, when = stage(1 + LAG)
+        u, when = stage(2 + LAG)
 
         @when
         def _(u=u):
@@ -345,7 +345,7 @@
 
         return 0
 
-    lax.fori_loop(0, units + 3 + 7 * LAG, step, 0)
+    lax.fori_loop(0, units + 4 + 7 * LAG, step, 0)
 
 
 def write(x, out, sems):

time: 282 us -> 282 us (level)
  no operation moved by 1% of the time
where the time goes in v4:
time: 282 us; the launch traced here: 281 us
  Pallas kernels  281 us (100%)
    pallas_call x1, Pallas kernels, local(): pl.pallas_call(body, out_shape=pltpu.VMEM((mats, depth, cols), BF16), in_...  271 us
    pallas_call x1, Pallas kernels, local(): pl.pallas_call(write, out_shape=jax.ShapeDtypeStruct((mats, depth, cols),...  10.4 us

profile of v4, /device:TPU:0, one launch (start us, length us, event | category | flops | bytes accessed | tf_op | source)
XLA Modules:
  0.0 281.5 jit_solution(2886570402925165860)
XLA Ops:
  0.0 271.0 %shard_map.28.x = bf16[4,1280,3072]{2,1,0:T(8,128)(2,1)S(1)} custom-call(bf16[1,4,4096,1280]{3,2,1,0:T(8,128)(2,1)} %refs_0_.1, bf16[1,4,4096,3072]{3,2,1,0:T(8,128)(2,1)} %refs_1_.1), custom_call_target="tpu_custom_call" | custom-call | flops 128849018880 | bytes 142606336 | tf_op jit(solution)/shard_map/pallas_call | solution.py:379
  271.0 10.4 %shard_map.29 = bf16[4,1280,3072]{2,1,0:T(8,128)(2,1)} custom-call(bf16[4,1280,3072]{2,1,0:T(8,128)(2,1)S(1)} %shard_map.28.x), custom_call_target="tpu_custom_call" | custom-call | tf_op jit(solution)/shard_map/pallas_call | solution.py:402
